TPU v7x, 256 devices: a whole 4x4x8 slice. The times are simulated.
256 devices in a mesh: section: 8 (over x, core), ep: 32 (over y, z).
Axes of the slice: x: 4, y: 4, z: 8, core: 2. Of those that a mesh axis runs over, the one named last changes fastest.
Arguments:
- hidden_states: bfloat16 [1536, 6144], P('ep'), may hold values from -6 to 6
- route_experts: int32 [1536, 2], P('ep'), may hold values from 0 to 7, all different within a row; in each aligned block of 48 rows (0 to 47, 48 to 95, ...) at most 24 rows name the same one
- route_weights: float32 [1536, 2], P('ep'), may hold values from 0.05 to 1
- gate_weight: bfloat16 [32, 6144, 2048], P('ep', None, 'section'), may hold values from -0.078125 to 0.078125
- up_weight: bfloat16 [32, 6144, 2048], P('ep', None, 'section'), may hold values from -0.078125 to 0.078125
- down_weight: bfloat16 [32, 2048, 6144], P('ep', 'section'), may hold values from -0.0625 to 0.0625
Outputs:
- layer_out: bfloat16 [1536, 6144], P('ep', 'section')
Inputs may be any that keep to these rules, and one draw needn't show every extreme that they name: `route_experts`: each row names two different experts. Among the 48 rows of one ep index no expert is named by more than 24 rows, and in every draw some expert is named by exactly 24 rows of some ep index.
All inputs are finite; a program needn't handle non-finite values.
Results may differ from a plain program's by a relative error of at most 0.015.
Values may be sent and summed in bfloat16 or wider, within the bound.
A program may use at most 128 MiB of HBM per device.

v0:
```python
import jax
import jax.numpy as jnp
from jax import lax
from jax.sharding import PartitionSpec as P

EXPERTS = 8


def cut_along(x, dim, peers):
    before, after = (x.shape[:dim], x.shape[dim + 1 :])
    return jnp.moveaxis(x.reshape(*before, peers, -1, *after), dim, 0)


def sent_and_summed(x, axis, dim):
    peers = lax.axis_size(axis)
    parts = lax.all_to_all(cut_along(x, dim, peers), axis, 0, 0, tiled=True)
    return jnp.sum(parts.astype(jnp.float32), axis=0)


def expert_rows(incoming, gate_weight, up_weight, down_weight):
    sources, slot_count, features = incoming.shape
    stacked = incoming.reshape(sources * slot_count, features)
    gate_value = jnp.dot(stacked, gate_weight[0], preferred_element_type=jnp.float32)
    up_value = jnp.dot(stacked, up_weight[0], preferred_element_type=jnp.float32)
    hidden = (jax.nn.silu(gate_value) * up_value).astype(jnp.bfloat16)
    result = jnp.dot(hidden, down_weight[0], preferred_element_type=jnp.float32).astype(
        jnp.bfloat16
    )
    return result.reshape(sources, slot_count, features)


def on_device(hidden_states, route_experts, route_weights, gate_weight, up_weight, down_weight):
    ep_count = lax.axis_size("ep")
    section_count = lax.axis_size("section")
    tok_rows, features = hidden_states.shape
    members = ep_count // EXPERTS
    capacity = tok_rows // 2
    chosen = route_experts.reshape(-1)
    one_hot = (chosen[:, None] == jnp.arange(EXPERTS, dtype=jnp.int32)[None, :]).astype(jnp.int32)
    earlier = jnp.cumsum(one_hot, axis=0) - one_hot
    slot_index = jnp.sum(earlier * one_hot, axis=1)
    position = (chosen * capacity + slot_index).reshape(tok_rows, 2)
    columns = jnp.arange(EXPERTS * capacity, dtype=jnp.int32)
    matches = position[:, :, None] == columns[None, None, :]
    select = jnp.sum(matches.astype(jnp.int32), axis=1).astype(jnp.bfloat16)
    weighing = jnp.sum(matches.astype(jnp.float32) * route_weights[:, :, None], axis=1)
    packed = jnp.einsum(
        "tj,td->jd", select, hidden_states, preferred_element_type=jnp.float32
    ).astype(jnp.bfloat16)
    outgoing = jnp.repeat(packed.reshape(EXPERTS, capacity, features), members, axis=0)
    slot_share = capacity // section_count
    first_slot = lax.axis_index("section") * slot_share
    own_slots = lax.dynamic_slice_in_dim(outgoing, first_slot, slot_share, 1)
    arrived = lax.all_to_all(own_slots, "ep", split_axis=0, concat_axis=0, tiled=True)
    partials = expert_rows(
        lax.all_gather(arrived, "section", axis=1, tiled=True), gate_weight, up_weight, down_weight
    )
    summed = lax.psum_scatter(
        partials.astype(jnp.float32).astype(jnp.bfloat16),
        "section",
        scatter_dimension=1,
        tiled=True,
    ).astype(jnp.float32)
    returned = lax.all_to_all(
        summed.astype(jnp.bfloat16), "ep", split_axis=0, concat_axis=0, tiled=True
    ).astype(summed.dtype)
    merged = jnp.sum(returned.reshape(EXPERTS, members, slot_share, features), axis=1)
    weigh_part = lax.dynamic_slice_in_dim(
        weighing.reshape(tok_rows, EXPERTS, capacity), first_slot, slot_share, 2
    )
    contribution = jnp.dot(
        weigh_part.reshape(tok_rows, EXPERTS * slot_share),
        merged.reshape(EXPERTS * slot_share, features),
        preferred_element_type=jnp.float32,
    )
    layer_out = sent_and_summed(contribution.astype(jnp.bfloat16), "section", 1)
    return layer_out.astype(jnp.bfloat16)


def solution(mesh):
    return jax.shard_map(
        on_device,
        mesh=mesh,
        in_specs=(
            P("ep", None),
            P("ep", None),
            P("ep", None),
            P("ep", None, "section"),
            P("ep", None, "section"),
            P("ep", "section", None),
        ),
        out_specs=P("ep", "section"),
        check_vma=False,
    )
```

profile of v0, /device:TPU:1, one launch (start us, length us, event | category | flops | bytes accessed | tf_op | source)
XLA Modules:
  0.0 317.6 jit_solution(11855568616730549436)
XLA Ops:
  6.5 0.9 copy.60
  7.5 0.1 eq.28
  7.6 0.1 fusion.21
  7.7 0.1 reduce_window_sum.11
  7.8 0.2 select_reduce_fusion.1
  8.0 0.1 reduce_sum.51
  8.1 0.1 copy.61
  8.2 0.7 multiply_add_fusion
  8.9 0.1 convert_reduce_fusion.1
  9.0 1.9 convolution_convert_fusion.1
  10.8 4.8 %broadcast_in_dim.2 = bf16[8,4,24,6144]{3,2,1,0:T(8,128)(2,1)} broadcast(bf16[8,24,6144]{2,1,0:T(8,128)(2,1)S(1)} %bitcast.41), dimensions={0,2,3} | broadcast | bytes 11796480 | tf_op jit(solution)/shard_map/broadcast_in_dim | solution.py:50
  15.6 4.0 %constant_dynamic-slice_fusion.1 = bf16[32,3,6144]{2,1,0:T(4,128)(2,1)S(1)} fusion(bf16[32,24,6144]{2,1,0:T(8,128)(2,1)} %bitcast.37, s32[]{:T(128)S(6)} %select_n.4), kind=kLoop, calls=%fused_computation.30 | loop fusion | bytes 2359300 | tf_op jit(solution)/shard_map/dynamic_slice | solution.py:53
  19.6 48.3 %all_to_all.15 = bf16[32,3,6144]{2,1,0:T(4,128)(2,1)S(1)} all-to-all(bf16[32,3,6144]{2,1,0:T(4,128)(2,1)S(1)} %constant_dynamic-slice_fusion.1), channel_id=1, replica_groups=mesh['section'=8,'ep'=32] {'ep'}, dimensions={0} | all-to-all | bytes 2359296 | tf_op jit(solution)/shard_map/all_to_all | solution.py:54
  67.9 1.9 copy.64
  69.8 0.0 all-gather.2.cloned.1.call-update
  69.8 0.2 reduce-scatter.2.cloned.1.call-start
  70.0 57.2 %all-gather.2.cloned.1.call-done = bf16[32,24,6144]{2,0,1:T(8,128)(2,1)} async-done(((bf16[32,3,6144]{2,0,1:T(8,128)(2,1)}), bf16[32,24,6144]{2,0,1:T(8,128)(2,1)}) %all-gather.2.cloned.1.call-update) | async-done | bytes 9437200 | tf_op jit(solution)/shard_map/all_gather | solution.py:56
  127.2 12.5 %copy.65 = bf16[32,24,6144]{2,1,0:T(8,128)(2,1)} copy(bf16[32,24,6144]{2,0,1:T(8,128)(2,1)} %all-gather.2.cloned.1.call-done) | data formatting | bytes 18874368 | tf_op jit(solution)/shard_map/all_gather | solution.py:56
  139.7 8.1 %fusion.4 = f32[768,256]{1,0:T(8,128)} fusion(bf16[768,6144]{1,0:T(8,128)(2,1)} %bitcast.38, bf16[1,6144,256]{2,1,0:T(8,128)(2,1)} %param.9), kind=kOutput, calls=%fused_computation.8 | convolution fusion | flops 2415919104 | bytes 13369344 | tf_op jit(solution)/shard_map/dot_general | solution.py:23
  147.7 19.4 %convolution_convert_fusion = bf16[768,6144]{1,0:T(8,128)(2,1)} fusion(bf16[1,256,6144]{2,1,0:T(8,128)(2,1)S(1)} %copy-done, bf16[768,6144]{1,0:T(8,128)(2,1)} %bitcast.39, bf16[1,6144,256]{2,1,0:T(8,128)(2,1)} %param.10, f32[768,256]{1,0:T(8,128)} %fusion.4), kind=kOutput, calls=%fused_computation | convolution fusion | flops 4837736448 | bytes 25952256 | tf_op jit(solution)/shard_map/dot_general | solution.py:26
  167.1 12.5 %copy.66 = bf16[32,24,6144]{2,0,1:T(8,128)(2,1)} copy(bf16[32,24,6144]{2,1,0:T(8,128)(2,1)} %bitcast.40) | data formatting | bytes 18874368 | tf_op jit(solution)/shard_map/reshape | solution.py:29
  179.6 0.0 reduce-scatter.2.cloned.1.call-update
  179.7 59.5 %reduce-scatter.2.cloned.1.call-done = bf16[32,3,6144]{2,0,1:T(8,128)(2,1)} async-done(((bf16[32,24,6144]{2,0,1:T(8,128)(2,1)}), bf16[32,3,6144]{2,0,1:T(8,128)(2,1)}) %reduce-scatter.2.cloned.1.call-update) | async-done | bytes 1179664 | tf_op jit(solution)/shard_map/reduce_scatter | solution.py:58
  239.1 3.4 %copy.67 = bf16[32,3,6144]{2,1,0:T(4,128)(2,1)} copy(bf16[32,3,6144]{2,0,1:T(8,128)(2,1)} %reduce-scatter.2.cloned.1.call-done) | data formatting | bytes 2359296 | tf_op jit(solution)/shard_map/reduce_scatter | solution.py:58
  242.5 9.7 %all-to-all-start.1 = ((bf16[32,3,6144]{2,1,0:T(4,128)(2,1)}), bf16[32,3,6144]{2,1,0:T(4,128)(2,1)}, u32[]{:S(2)}, u32[]{:S(2)}) async-start(bf16[32,3,6144]{2,1,0:T(4,128)(2,1)} %copy.67), calls=%async_computation.2 | async-start | bytes 3145728 | tf_op jit(solution)/shard_map/all_to_all | solution.py:64
  252.3 0.1 select_reduce_fusion
  252.4 0.1 copy.62
  252.5 36.7 %all-to-all-done.1 = bf16[32,3,6144]{2,1,0:T(4,128)(2,1)} async-done(((bf16[32,3,6144]{2,1,0:T(4,128)(2,1)}), bf16[32,3,6144]{2,1,0:T(4,128)(2,1)}, u32[]{:S(2)}, u32[]{:S(2)}) %all-to-all-start.1) | async-done | bytes 1179680 | tf_op jit(solution)/shard_map/all_to_all | solution.py:64
  289.2 2.4 convert_reduce_fusion
  291.5 0.4 fusion
  292.0 17.0 %all_to_all.16 = bf16[8,48,768]{2,1,0:T(8,128)(2,1)} all-to-all(bf16[8,48,768]{2,1,0:T(8,128)(2,1)S(1)} %bitcast.43), channel_id=1, replica_groups=mesh['section'=8,'ep'=32] {'section'}, dimensions={0} | all-to-all | bytes 1179648 | tf_op jit(solution)/shard_map/all_to_all | solution.py:16
  308.9 1.8 reduce_sum.55
  (9 shorter events, 0.1 us)
Async XLA Ops:
  6.5 141.2 %copy-start = (bf16[1,256,6144]{2,1,0:T(8,128)(2,1)S(1)}, bf16[1,256,6144]{2,1,0:T(8,128)(2,1)}, u32[]{:S(2)}) copy-start(bf16[1,256,6144]{2,1,0:T(8,128)(2,1)} %param.11) | copy-start | bytes 9437188
  6.5 120.6 %all-gather.2.cloned.1.call-start = ((), (), s32[]{:S(2)}) async-start(), calls=%async_computation.4 | async-start | bytes 10616832 | tf_op jit(solution)/shard_map/all_gather | solution.py:56
  69.8 169.3 %reduce-scatter.2.cloned.1.call-start = ((), (), s32[]{:S(2)}) async-start(), calls=%async_computation.5 | async-start | bytes 10616832 | tf_op jit(solution)/shard_map/reduce_scatter | solution.py:58
  179.6 72.6 %copy-start.2 = (f32[48,2]{0,1:T(2,128)S(1)}, f32[48,2]{0,1:T(2,128)}, u32[]{:S(2)}) copy-start(f32[48,2]{0,1:T(2,128)} %param.8) | copy-start | bytes 1156
  242.5 46.6 %all-to-all-start.1 = ((bf16[32,3,6144]{2,1,0:T(4,128)(2,1)}), bf16[32,3,6144]{2,1,0:T(4,128)(2,1)}, u32[]{:S(2)}, u32[]{:S(2)}) async-start(bf16[32,3,6144]{2,1,0:T(4,128)(2,1)} %copy.67), calls=%async_computation.2 | async-start | bytes 3145728 | tf_op jit(solution)/shard_map/all_to_all | solution.py:64
  252.2 58.5 %copy-start.1 = (bf16[1,256,6144]{2,1,0:T(8,128)(2,1)S(1)}, bf16[1,256,6144]{2,1,0:T(8,128)(2,1)}, u32[]{:S(2)}) copy-start(bf16[1,256,6144]{2,1,0:T(8,128)(2,1)} %param.11) | copy-start | bytes 9437188
Sparse Core Ops, SparseCore 0:
  69.9 57.2 all-gather.1
  179.8 59.3 reduce-scatter.1
where the time goes:
time: 318 us
  waiting for transfers between devices  153 us (48%)
  blocking collectives  65.3 us (21%)
  local copies, waits for them, and re-layouts  40.4 us (13%)
  matrix products  29.7 us (9%)
  between operations  13.5 us (4%)
  starting transfers between devices  9.91 us (3%)
  other arithmetic  5.43 us (2%)
    reduce_scatter x1, waiting for transfers between devices, on_device(): lax.psum_scatter(partials.astype(jnp.float32).astype(jnp.bfloat16), 'sect...  59.5 us
    all_gather x1, waiting for transfers between devices, on_device(): lax.all_gather(arrived, 'section', axis=1, tiled=True)  57.2 us
    all_to_all x1, blocking collectives, on_device(): lax.all_to_all(own_slots, 'ep', split_axis=0, concat_axis=0, tiled=True)  48.3 us
    all_to_all x1, waiting for transfers between devices, on_device(): lax.all_to_all(summed.astype(jnp.bfloat16), 'ep', split_axis=0, concat_ax...  36.7 us
    dot_general x1, matrix products, expert_rows(): jnp.dot(hidden, down_weight[0], preferred_element_type=jnp.float32)  19.4 us
    all_to_all x1, blocking collectives, sent_and_summed(): parts = lax.all_to_all(cut_along(x, dim, peers), axis, 0, 0, tiled=True)  17 us
    reshape x1, local copies, waits for them, and re-layouts, expert_rows(): return result.reshape(sources, slot_count, features)  12.5 us
    all_gather x1, local copies, waits for them, and re-layouts, on_device(): lax.all_gather(arrived, 'section', axis=1, tiled=True)  12.5 us
  transfers between devices with their start and end apart: 3, of which 3 were waited for; matrix products, arithmetic and copies ran while one was open for 0% of the time, Pallas kernels for 0%

commit v1 on v0

--- a/solution.py
+++ b/solution.py
@@ -53,7 +53,12 @@
     own_slots = lax.dynamic_slice_in_dim(outgoing, first_slot, slot_share, 1)
     arrived = lax.all_to_all(own_slots, "ep", split_axis=0, concat_axis=0, tiled=True)
     partials = expert_rows(
-        lax.all_gather(arrived, "section", axis=1, tiled=True), gate_weight, up_weight, down_weight
+        jnp.concatenate(
+            lax.all_to_all(jnp.stack([arrived] * lax.axis_size("section")), "section", 0, 0), axis=1
+        ),
+        gate_weight,
+        up_weight,
+        down_weight,
     )
     summed = lax.psum_scatter(
         partials.astype(jnp.float32).astype(jnp.bfloat16),

time: 318 us -> 408 us (1.28)
  blocking collectives: 65.3 us -> 178 us
  waiting for transfers between devices: 153 us -> 92.7 us
  local copies, waits for them, and re-layouts: 40.4 us -> 78.4 us
    all_to_all x0 -> x1, blocking collectives: none -> 113 us  [on_device(): lax.all_to_all(jnp.stack([arrived] * lax.axis_size('section')), 'section'...]
    all_gather x1 -> x0, waiting for transfers between devices: 57.2 us -> none  [on_device(): lax.all_gather(arrived, 'section', axis=1, tiled=True)]
    reshape x0 -> x1, local copies, waits for them, and re-layouts: none -> 26.7 us  [on_device(): jnp.concatenate(lax.all_to_all(jnp.stack([arrived] * lax.axis_size('secti...]
    another operation x0 -> x2, local copies, waits for them, and re-layouts: none -> 24.7 us  [the longest x1 23.5 us: expert_rows(): stacked = incoming.reshape(sources * slot_count, features)]
    all_gather x1 -> x0, local copies, waits for them, and re-layouts: 12.5 us -> none  [on_device(): lax.all_gather(arrived, 'section', axis=1, tiled=True)]
  transfers between devices with their start and end apart: 3 -> 2, of which waited for: 3 -> 2; matrix products, arithmetic and copies ran while one was open for 0% -> 0% of each run, Pallas kernels for 0% -> 0%
where the time goes in v1:
time: 408 us; the launch traced here: 407 us
  blocking collectives  178 us (44%)
  waiting for transfers between devices  92.7 us (23%)
  local copies, waits for them, and re-layouts  78.4 us (19%)
  matrix products  29.7 us (7%)
  between operations  13.5 us (3%)
  starting transfers between devices  9.68 us (2%)
  other arithmetic  5.43 us (1%)
    all_to_all x1, blocking collectives, on_device(): lax.all_to_all(jnp.stack([arrived] * lax.axis_size('section')), 'section'...  113 us
    reduce_scatter x1, waiting for transfers between devices, on_device(): lax.psum_scatter(partials.astype(jnp.float32).astype(jnp.bfloat16), 'sect...  56 us
    all_to_all x1, blocking collectives, on_device(): lax.all_to_all(own_slots, 'ep', split_axis=0, concat_axis=0, tiled=True)  48.3 us
    all_to_all x1, waiting for transfers between devices, on_device(): lax.all_to_all(summed.astype(jnp.bfloat16), 'ep', split_axis=0, concat_ax...  36.7 us
    reshape x1, local copies, waits for them, and re-layouts, on_device(): jnp.concatenate(lax.all_to_all(jnp.stack([arrived] * lax.axis_size('secti...  26.7 us
    another operation x1, local copies, waits for them, and re-layouts, expert_rows(): stacked = incoming.reshape(sources * slot_count, features)  23.5 us
    dot_general x1, matrix products, expert_rows(): jnp.dot(hidden, down_weight[0], preferred_element_type=jnp.float32)  19.4 us
    all_to_all x1, blocking collectives, sent_and_summed(): parts = lax.all_to_all(cut_along(x, dim, peers), axis, 0, 0, tiled=True)  16.9 us
  transfers between devices with their start and end apart: 2, of which 2 were waited for; matrix products, arithmetic and copies ran while one was open for 0% of the time, Pallas kernels for 0%

profile of v1, /device:TPU:1, one launch (start us, length us, event | category | flops | bytes accessed | tf_op | source)
XLA Modules:
  0.0 407.2 jit_solution(217330912048742869)
XLA Ops:
  6.5 0.9 copy.50
  7.5 0.1 eq.28
  7.6 0.1 fusion.21
  7.7 0.1 reduce_window_sum.11
  7.8 0.2 select_reduce_fusion.1
  8.0 0.1 reduce_sum.51
  8.1 0.1 copy.51
  8.2 0.7 multiply_add_fusion
  8.9 0.1 convert_reduce_fusion.1
  9.0 1.9 convolution_convert_fusion.1
  10.8 4.8 %broadcast_in_dim.2 = bf16[8,4,24,6144]{3,2,1,0:T(8,128)(2,1)} broadcast(bf16[8,24,6144]{2,1,0:T(8,128)(2,1)S(1)} %bitcast.40), dimensions={0,2,3} | broadcast | bytes 11796480 | tf_op jit(solution)/shard_map/broadcast_in_dim | solution.py:50
  15.6 4.0 constant_dynamic-slice_fusion.1
  19.6 48.3 %all_to_all.20 = bf16[32,3,6144]{2,1,0:T(4,128)(2,1)S(1)} all-to-all(bf16[32,3,6144]{2,1,0:T(4,128)(2,1)S(1)} %constant_dynamic-slice_fusion.1), channel_id=1, replica_groups=mesh['section'=8,'ep'=32] {'ep'}, dimensions={0} | all-to-all | bytes 2359296 | tf_op jit(solution)/shard_map/all_to_all | solution.py:54
  67.9 0.9 copy.54
  68.8 1.2 stack.2
  69.9 112.6 %all_to_all.21 = bf16[8,32,3,6144]{3,1,2,0:T(8,128)(2,1)S(1)} all-to-all(bf16[8,32,3,6144]{3,1,2,0:T(8,128)(2,1)S(1)} %stack.2), channel_id=1, replica_groups=mesh['section'=8,'ep'=32] {'section'}, dimensions={0} | all-to-all | bytes 18874368 | tf_op jit(solution)/shard_map/all_to_all | solution.py:57
  182.6 26.7 %copy.55 = bf16[32,8,3,6144]{3,2,1,0:T(4,128)(2,1)} copy(bf16[32,8,3,6144]{3,0,2,1:T(8,128)(2,1)S(1)} %bitcast.37) | data formatting | bytes 18874368 | tf_op jit(solution)/shard_map/reshape | solution.py:56
  209.3 23.5 %reshape_reshape.3 = bf16[768,6144]{1,0:T(8,128)(2,1)} reshape(bf16[32,8,3,6144]{3,2,1,0:T(4,128)(2,1)} %copy.55) | data formatting | bytes 18874368 | tf_op jit(solution)/shard_map/reshape;reshape | solution.py:22
  232.8 8.1 %fusion.4 = f32[768,256]{1,0:T(8,128)} fusion(bf16[768,6144]{1,0:T(8,128)(2,1)} %reshape_reshape.3, bf16[1,6144,256]{2,1,0:T(8,128)(2,1)} %param.9), kind=kOutput, calls=%fused_computation.8 | convolution fusion | flops 2415919104 | bytes 13369344 | tf_op jit(solution)/shard_map/dot_general | solution.py:23
  240.9 19.4 %convolution_convert_fusion = bf16[768,6144]{1,0:T(8,128)(2,1)} fusion(bf16[1,256,6144]{2,1,0:T(8,128)(2,1)S(1)} %copy-done, bf16[768,6144]{1,0:T(8,128)(2,1)} %reshape_reshape.3, bf16[1,6144,256]{2,1,0:T(8,128)(2,1)} %param.10, f32[768,256]{1,0:T(8,128)} %fusion.4), kind=kOutput, calls=%fused_computation | convolution fusion | flops 4837736448 | bytes 25952256 | tf_op jit(solution)/shard_map/dot_general | solution.py:26
  260.3 12.5 %copy.56 = bf16[32,24,6144]{2,0,1:T(8,128)(2,1)} copy(bf16[32,24,6144]{2,1,0:T(8,128)(2,1)} %bitcast.39) | data formatting | bytes 18874368 | tf_op jit(solution)/shard_map/reshape | solution.py:29
  272.8 0.0 reduce-scatter.2.cloned.1.call-update
  272.8 56.0 %reduce-scatter.2.cloned.1.call-done = bf16[32,3,6144]{2,0,1:T(8,128)(2,1)} async-done(((bf16[32,24,6144]{2,0,1:T(8,128)(2,1)}), bf16[32,3,6144]{2,0,1:T(8,128)(2,1)}) %reduce-scatter.2.cloned.1.call-update) | async-done | bytes 1179664 | tf_op jit(solution)/shard_map/reduce_scatter | solution.py:63
  328.7 3.4 copy.57
  332.2 9.7 %all-to-all-start.2 = ((bf16[32,3,6144]{2,1,0:T(4,128)(2,1)}), bf16[32,3,6144]{2,1,0:T(4,128)(2,1)}, u32[]{:S(2)}, u32[]{:S(2)}) async-start(bf16[32,3,6144]{2,1,0:T(4,128)(2,1)} %copy.57), calls=%async_computation.3 | async-start | bytes 3145728 | tf_op jit(solution)/shard_map/all_to_all | solution.py:69
  341.9 0.1 select_reduce_fusion
  342.0 0.1 copy.52
  342.1 36.7 %all-to-all-done.2 = bf16[32,3,6144]{2,1,0:T(4,128)(2,1)} async-done(((bf16[32,3,6144]{2,1,0:T(4,128)(2,1)}), bf16[32,3,6144]{2,1,0:T(4,128)(2,1)}, u32[]{:S(2)}, u32[]{:S(2)}) %all-to-all-start.2) | async-done | bytes 1179680 | tf_op jit(solution)/shard_map/all_to_all | solution.py:69
  378.8 2.4 convert_reduce_fusion
  381.2 0.4 fusion
  381.6 16.9 %all_to_all.22 = bf16[8,48,768]{2,1,0:T(8,128)(2,1)} all-to-all(bf16[8,48,768]{2,1,0:T(8,128)(2,1)S(1)} %bitcast.42), channel_id=1, replica_groups=mesh['section'=8,'ep'=32] {'section'}, dimensions={0} | all-to-all | bytes 1179648 | tf_op jit(solution)/shard_map/all_to_all | solution.py:16
  398.6 1.8 reduce_sum.55
  (7 shorter events, 0.1 us)
Async XLA Ops:
  6.5 234.3 %copy-start = (bf16[1,256,6144]{2,1,0:T(8,128)(2,1)S(1)}, bf16[1,256,6144]{2,1,0:T(8,128)(2,1)}, u32[]{:S(2)}) copy-start(bf16[1,256,6144]{2,1,0:T(8,128)(2,1)} %param.11) | copy-start | bytes 9437188
  6.5 322.2 %reduce-scatter.2.cloned.1.call-start = ((), (), s32[]{:S(2)}) async-start(), calls=%async_computation.5 | async-start | bytes 10616832 | tf_op jit(solution)/shard_map/reduce_scatter | solution.py:63
  272.8 69.1 %copy-start.1 = (f32[48,2]{0,1:T(2,128)S(1)}, f32[48,2]{0,1:T(2,128)}, u32[]{:S(2)}) copy-start(f32[48,2]{0,1:T(2,128)} %param.8) | copy-start | bytes 1156
  332.2 46.7 %all-to-all-start.2 = ((bf16[32,3,6144]{2,1,0:T(4,128)(2,1)}), bf16[32,3,6144]{2,1,0:T(4,128)(2,1)}, u32[]{:S(2)}, u32[]{:S(2)}) async-start(bf16[32,3,6144]{2,1,0:T(4,128)(2,1)} %copy.57), calls=%async_computation.3 | async-start | bytes 3145728 | tf_op jit(solution)/shard_map/all_to_all | solution.py:69
Sparse Core Ops, SparseCore 0:
  272.9 55.8 reduce-scatter.1
